TPU v7x, 32 devices: a whole 2x2x4 slice. The times are simulated.
32 devices in a mesh: groups: 2 (over x), attn: 4 (over y, core), expert: 4 (over z).
Axes of the slice: x: 2, y: 2, z: 4, core: 2. Of those that a mesh axis runs over, the one named last changes fastest.
Arguments:
- tokens: bfloat16 [1024, 4096], P(('groups', 'attn'), 'expert'), parts along dimension 0, may hold values from -6 to 6
- expert_ids: int32 [1024, 8], P(('groups', 'attn')), parts along dimension 0, may hold values from 0 to 15, all different within a row; in each aligned block of 128 rows (0 to 127, 128 to 255, ...) at most 128 rows name the same one
- gate_weight: bfloat16 [1024, 8], P(('groups', 'attn')), parts along dimension 0, may hold values from 0.049804688 to 0.29882812
- w_gate: bfloat16 [16, 4096, 768], P('attn', 'expert'), may hold values from -0.09375 to 0.09375
- w_up: bfloat16 [16, 4096, 768], P('attn', 'expert'), may hold values from -0.09375 to 0.09375
- w_down: bfloat16 [16, 768, 4096], P('attn', None, 'expert'), may hold values from -0.21875 to 0.21875
- query: bfloat16 [64, 64, 128], P(('groups', 'attn', 'expert')), parts along dimension 0, may hold values from -100 to 100
- cache_k: bfloat16 [64, 768, 4, 128], P(('groups', 'attn', 'expert')), parts along dimension 0, may hold values from -6 to 6
- cache_v: bfloat16 [64, 768, 4, 128], P(('groups', 'attn', 'expert')), parts along dimension 0, may hold values from -6 to 6
- lengths: int32 [64], P(('groups', 'attn', 'expert')), parts along dimension 0, may hold values from 2 to 768, as said below
Outputs:
- moe_out: bfloat16 [1024, 4096], P(('groups', 'attn'), 'expert'), parts along dimension 0
- attn_out: bfloat16 [64, 8192], P(('groups', 'attn', 'expert')), parts along dimension 0
There are 2 independent parts, one for each index of `groups`. A program takes and returns all parts, laid end to end along the dimension named above; an argument that names none is the same for every part. Nothing has to cross between parts.
Inputs may be any that keep to these rules, and one draw needn't show every extreme that they name: `expert_ids`: each row names 8 different experts. In the rows of one index of attn (aligned blocks of 128 rows) no expert is named by more than 128 rows, and in some block some expert by exactly 128. `lengths`: some sequence has all 768 positions live.
All inputs are finite; a program needn't handle non-finite values.
Results may differ from a plain program's by a relative error of at most 0.025.
Values may be sent and summed in bfloat16 or wider, within the bound.
A program may use at most 64 MiB of HBM per device.

v0:
```python
import jax
import jax.numpy as jnp
from jax import lax
from jax.sharding import PartitionSpec as P


def member_table(expert_ids, experts):
    wanted = jnp.arange(experts, dtype=jnp.int32)
    return jnp.any(expert_ids[:, :, None] == wanted[None, None, :], axis=1).astype(jnp.int32)


def pad_rows(values):
    feat_width = values.shape[-1]
    flat_rows = values.reshape(-1, feat_width)
    return jnp.concatenate([flat_rows, jnp.zeros((1, feat_width), values.dtype)], axis=0)


def return_slots(results, starts_in, kept_in, slot_count):
    local_experts = results.shape[0]
    capacity = results.shape[1]
    slot_ids = jnp.arange(slot_count, dtype=jnp.int32)[None, None, :]
    column = jnp.arange(local_experts, dtype=jnp.int32)[None, :, None]
    row_index = column * capacity + starts_in[:, :, None] + slot_ids
    row_index = jnp.where(slot_ids < kept_in[:, :, None], row_index, local_experts * capacity)
    return pad_rows(results)[row_index]


def grouped_attention(query, cache_k, cache_v, lengths):
    seq_count, head_total, head_size = query.shape
    context = cache_k.shape[1]
    kv_count = cache_k.shape[2]
    grouped = query.reshape(seq_count, kv_count, head_total // kv_count, head_size)
    scores = jnp.einsum(
        "skgd,slkd->skgl", grouped, cache_k, preferred_element_type=jnp.float32
    ) * head_size ** (-0.5)
    live_mask = (
        lax.broadcasted_iota(jnp.int32, (seq_count, 1, 1, context), 3)
        < lengths[:, None, None, None]
    )
    masked = jnp.where(live_mask, scores, -jnp.inf)
    row_peak = jnp.max(masked, axis=3, keepdims=True)
    weighted = jnp.exp(masked - row_peak)
    denominator = jnp.sum(weighted, axis=3, keepdims=True)
    prob_bf = (weighted / denominator).astype(jnp.bfloat16)
    attended = jnp.einsum("skgl,slkd->skgd", prob_bf, cache_v, preferred_element_type=jnp.float32)
    return attended.reshape(seq_count, head_total * head_size).astype(jnp.bfloat16)


def body(tokens, expert_ids, gate_weight, w_gate, w_up, w_down, query, cache_k, cache_v, lengths):
    tok_rows, feat_width = tokens.shape
    top_count = expert_ids.shape[1]
    local_experts = w_gate.shape[0]
    ffn_width = w_gate.shape[2]
    attn_count = lax.axis_size("attn")
    experts = local_experts * attn_count
    capacity = tok_rows * top_count // local_experts
    slot_count = min(tok_rows, 3 * tok_rows * top_count // experts)
    member = member_table(expert_ids, experts)
    local_rank = jnp.cumsum(member, axis=0, dtype=jnp.int32) - member
    whole_ids = None
    whole_tokens, whole_ids, whole_gates = (
        lax.all_gather(tokens, "attn", axis=0, tiled=True),
        lax.all_gather(expert_ids, "attn", axis=0, tiled=True),
        lax.all_gather(gate_weight, "attn", axis=0, tiled=True),
    )
    all_rows = whole_tokens.shape[0]
    whole_member = member_table(whole_ids, experts)
    all_counts = jnp.sum(
        whole_member.reshape(attn_count, tok_rows, experts), axis=1, dtype=jnp.int32
    )
    src_offsets = jnp.cumsum(all_counts, axis=0, dtype=jnp.int32) - all_counts
    src_kept = jnp.clip(capacity - src_offsets, 0, all_counts)
    my_index = lax.axis_index("attn")
    offsets = lax.dynamic_index_in_dim(src_offsets, my_index, 0, keepdims=False)
    position = offsets[None, :] + local_rank
    starts_in = lax.dynamic_slice_in_dim(src_offsets, my_index * local_experts, local_experts, 1)
    kept_in = lax.dynamic_slice_in_dim(src_kept, my_index * local_experts, local_experts, 1)
    my_member = lax.dynamic_slice_in_dim(whole_member, my_index * local_experts, local_experts, 1)
    queue_place = jnp.cumsum(my_member, axis=0, dtype=jnp.int32) - my_member
    pack_target = jnp.where(
        (my_member > 0) & (queue_place < capacity),
        jnp.arange(local_experts, dtype=jnp.int32)[None, :] * capacity + queue_place,
        local_experts * capacity,
    )
    holders = jnp.broadcast_to(
        jnp.arange(all_rows, dtype=jnp.int32)[:, None], (all_rows, local_experts)
    )
    pack_index = (
        jnp.full((local_experts * capacity,), all_rows, jnp.int32)
        .at[pack_target.reshape(-1)]
        .set(holders.reshape(-1), mode="drop")
    )
    packed = pad_rows(whole_tokens)[pack_index].reshape(local_experts, capacity, feat_width)
    gate_part = jnp.einsum("jrd,jdf->jrf", packed, w_gate, preferred_element_type=jnp.float32)
    up_part = jnp.einsum("jrd,jdf->jrf", packed, w_up, preferred_element_type=jnp.float32)
    both_parts = jnp.concatenate([gate_part, up_part], axis=2)
    both_sums = lax.psum(both_parts.astype(jnp.bfloat16), "expert").astype(jnp.float32)
    hidden = (jax.nn.silu(both_sums[:, :, :ffn_width]) * both_sums[:, :, ffn_width:]).astype(
        jnp.bfloat16
    )
    results = jnp.einsum("jrf,jfd->jrd", hidden, w_down, preferred_element_type=jnp.float32).astype(
        jnp.bfloat16
    )
    back_rows = return_slots(results, starts_in, kept_in, slot_count)
    returned = lax.all_to_all(back_rows, "attn", split_axis=0, concat_axis=0, tiled=True)
    slot_of = jnp.take_along_axis(local_rank, expert_ids, axis=1)
    place_of = jnp.take_along_axis(position, expert_ids, axis=1)
    keep_mask = place_of < capacity
    picked = returned.reshape(experts * slot_count, feat_width)[expert_ids * slot_count + slot_of]
    factor = jnp.where(keep_mask, gate_weight.astype(jnp.float32), 0.0)
    moe_out = jnp.sum(factor[:, :, None] * picked.astype(jnp.float32), axis=1).astype(jnp.bfloat16)
    attn_out = grouped_attention(query, cache_k, cache_v, lengths)
    return (moe_out, attn_out)


def solution(mesh):
    return jax.shard_map(
        body,
        mesh=mesh,
        in_specs=(
            P(("groups", "attn"), "expert"),
            P(("groups", "attn"), None),
            P(("groups", "attn"), None),
            P("attn", "expert", None),
            P("attn", "expert", None),
            P("attn", None, "expert"),
            P(("groups", "attn", "expert"), None, None),
            P(("groups", "attn", "expert"), None, None, None),
            P(("groups", "attn", "expert"), None, None, None),
            P(("groups", "attn", "expert")),
        ),
        out_specs=(P(("groups", "attn"), "expert"), P(("groups", "attn", "expert"), None)),
        check_vma=False,
    )
```

profile of v0, /device:TPU:1, one launch (start us, length us, event | category | flops | bytes accessed | tf_op | source)
XLA Modules:
  0.0 262.3 jit_solution(12744865341679624601)
XLA Ops:
  7.2 0.0 copy-start
  7.2 0.0 all-gather.2.cloned.1.call-start
  7.2 0.7 all-gather.2.cloned.1.call-update
  7.9 0.0 all-reduce.4.cloned.1.call-start
  8.0 6.3 %all_gather.6 = s32[512,8]{0,1:T(8,128)S(1)} all-gather(s32[128,8]{0,1:T(8,128)} %param.13), channel_id=1, replica_groups=mesh['groups'=2,'attn'=4,'expert'=4] {'attn'}, dimensions={0}, use_global_device_ids=true | all-gather | bytes 20480 | tf_op jit(solution)/shard_map/all_gather | solution.py:63
  14.3 1.2 reduce-window.6
  15.5 0.2 slice_reduce_fusion
  15.8 0.2 reduce-window.9
  15.9 0.1 add_bitcast_fusion
  16.0 0.1 add_select_fusion
  16.1 0.2 copy.103
  16.2 0.2 reshape.138
  16.5 0.2 reshape.186
  16.6 8.0 %scatter_custom_fusion = s32[1024]{0:T(1024)S(1)} fusion(s32[2048]{0:T(1024)S(1)} %bitcast.56, s32[2048]{0:T(1024)S(1)} %reshape.186, s32[]{:T(128)} %constant.34.clone.1), kind=kCustom, calls=%fused_computation.57 | custom fusion | bytes 4100 | tf_op jit(solution)/shard_map/scatter | solution.py:91
  24.7 4.0 %all-gather.2.cloned.1.call-done = bf16[512,1024]{1,0:T(8,128)(2,1)} async-done(((bf16[128,1024]{1,0:T(8,128)(2,1)}), bf16[512,1024]{1,0:T(8,128)(2,1)}) %all-gather.2.cloned.1.call-update) | async-done | bytes 1048592 | tf_op jit(solution)/shard_map/all_gather | solution.py:62
  28.7 1.3 concatenate.10
  30.0 5.4 %gather_fusion = bf16[1024,1024]{1,0:T(8,128)(2,1)} fusion(bf16[513,1024]{1,0:T(8,128)(2,1)S(1)} %concatenate.10, s32[1024]{0:T(1024)S(1)} %fusion.24), kind=kCustom, calls=%fused_computation.2 | custom fusion | bytes 4198400 | tf_op jit(solution)/shard_map/gather | solution.py:93
  35.4 0.0 copy-start.1
  35.4 5.4 %convolution_convert_fusion.1 = bf16[4,256,768]{2,1,0:T(8,128)(2,1)S(1)} fusion(bf16[4,256,1024]{2,1,0:T(8,128)(2,1)} %bitcast.48, bf16[4,1024,768]{2,1,0:T(8,128)(2,1)} %param.16), kind=kOutput, calls=%fused_computation.13 | convolution fusion | flops 1611399168 | bytes 9961472 | tf_op jit(solution)/shard_map/jrd,jdf->jrf/dot_general | solution.py:95
  40.8 0.0 copy-done.1
  40.8 4.6 %convolution_convert_fusion.2 = bf16[4,256,768]{2,1,0:T(8,128)(2,1)S(1)} fusion(bf16[4,256,1024]{2,1,0:T(8,128)(2,1)S(1)} %bitcast.49, bf16[4,1024,768]{2,1,0:T(8,128)(2,1)} %param.15), kind=kOutput, calls=%fused_computation.14 | convolution fusion | flops 1611399168 | bytes 9961472 | tf_op jit(solution)/shard_map/jrd,jdf->jrf/dot_general | solution.py:94
  45.4 2.0 pad_maximum_fusion
  47.3 0.0 all-reduce.4.cloned.1.call-update
  47.4 0.3 reduce_sum.27
  47.7 0.2 reduce_window_sum.37
  47.9 0.1 dynamic-slice_minimum_fusion
  48.0 0.1 copy.104
  48.1 0.1 copy.105
  48.1 0.1 compare_select_fusion.1
  48.2 119.8 %all-reduce.4.cloned.1.call-done = bf16[4,256,1536]{2,1,0:T(8,128)(2,1)} async-done(((bf16[4,256,1536]{2,1,0:T(8,128)(2,1)}), bf16[4,256,1536]{2,1,0:T(8,128)(2,1)}) %all-reduce.4.cloned.1.call-update) | async-done | bytes 3145744 | tf_op jit(solution)/shard_map/psum | solution.py:97
  168.0 2.7 %convert_element_type.45 = f32[4,256,1536]{2,1,0:T(8,128)S(1)} convert(bf16[4,256,1536]{2,1,0:T(8,128)(2,1)} %all-reduce.4.cloned.1.call-done) | non-fusion elementwise | flops 1572864 | bytes 9437184 | tf_op jit(solution)/shard_map/convert_element_type | solution.py:97
  170.7 4.9 %convolution_convert_fusion = bf16[4,256,1024]{2,1,0:T(8,128)(2,1)S(1)} fusion(bf16[4,768,1024]{2,1,0:T(8,128)(2,1)} %param.17, f32[4,256,1536]{2,1,0:T(8,128)S(1)} %convert_element_type.45), kind=kOutput, calls=%fused_computation.12 | convolution fusion | flops 1616379904 | bytes 14680064 | tf_op jit(solution)/shard_map/jrf,jfd->jrd/dot_general | solution.py:101
  175.6 1.5 concatenate.12
  177.1 12.9 %gather_fusion.1 = bf16[2048,1024]{1,0:T(8,128)(2,1)} fusion(bf16[1025,1024]{1,0:T(8,128)(2,1)} %concatenate.12, s32[2048]{0:T(1024)S(1)} %broadcast_clamp_fusion), kind=kCustom, calls=%fused_computation.3 | custom fusion | bytes 8396800 | tf_op jit(solution)/shard_map/gather | solution.py:25
  190.0 0.0 copy-start.2
  190.0 5.8 %all-to-all-start = ((bf16[4,4,128,1024]{3,2,1,0:T(8,128)(2,1)}), bf16[4,4,128,1024]{3,2,1,0:T(8,128)(2,1)}, u32[]{:S(2)}, u32[]{:S(2)}) async-start(bf16[4,4,128,1024]{3,2,1,0:T(8,128)(2,1)} %bitcast.47), calls=%async_computation | async-start | bytes 8388608 | tf_op jit(solution)/shard_map/all_to_all | solution.py:105
  195.8 0.0 copy-done.2
  195.8 0.1 copy.99
  195.9 0.2 reduce_window_sum.38
  196.1 0.1 copy.100
  196.2 0.1 reshape.206
  196.3 0.2 dynamic-slice_reduce_fusion
  196.5 7.1 %gather_fusion.4 = s32[1024]{0:T(1024)S(1)} fusion(s32[128,16]{1,0:T(8,128)S(1)} %get-tuple-element.4, s32[1024]{0:T(1024)S(1)} %reshape.206), kind=kCustom, calls=%fused_computation.1.clone | custom fusion | bytes 16384 | tf_op jit(solution)/shard_map/jit(take_along_axis)/gather | solution.py:106
  203.6 0.1 reshape.214
  203.7 0.1 copy.108
  203.9 0.1 reshape.176
  204.0 0.0 copy-start.4
  204.0 0.0 copy-start.5
  204.0 0.0 copy-start.3
  204.0 7.1 %gather_fusion.3 = s32[1024]{0:T(1024)S(1)} fusion(s32[128,16]{1,0:T(8,128)S(1)} %get-tuple-element.3, s32[1024]{0:T(1024)S(1)} %reshape.206), kind=kCustom, calls=%fused_computation.clone | custom fusion | bytes 16384 | tf_op jit(solution)/shard_map/jit(take_along_axis)/gather | solution.py:107
  211.1 0.1 reshape.209
  211.2 0.0 copy-done.4
  211.2 0.1 copy.102
  211.3 0.0 copy-done.5
  211.3 0.1 iota_compare_fusion.3
  211.4 0.0 copy-done
  211.4 0.0 copy-done.3
  211.4 0.5 fusion.14
  211.9 0.2 fusion.29
  212.2 1.8 fusion.17
  214.0 0.7 copy.127
  214.7 28.4 %all-to-all-done = bf16[4,4,128,1024]{3,2,1,0:T(8,128)(2,1)} async-done(((bf16[4,4,128,1024]{3,2,1,0:T(8,128)(2,1)}), bf16[4,4,128,1024]{3,2,1,0:T(8,128)(2,1)}, u32[]{:S(2)}, u32[]{:S(2)}) %all-to-all-start) | async-done | bytes 4194336 | tf_op jit(solution)/shard_map/all_to_all | solution.py:105
  243.1 8.8 %gather_fusion.2 = bf16[1024,1024]{1,0:T(8,128)(2,1)} fusion(bf16[2048,1024]{1,0:T(8,128)(2,1)} %bitcast.8, s32[1024]{0:T(1024)S(1)} %broadcast_clamp_fusion.1), kind=kCustom, calls=%fused_computation.4 | custom fusion | bytes 4198400 | tf_op jit(solution)/shard_map/gather | solution.py:109
  251.8 3.7 %fusion.1 = bf16[128,1024]{1,0:T(8,128)(2,1)} fusion(bf16[1024,1024]{1,0:T(8,128)(2,1)} %gather_fusion.2, f32[128,8]{1,0:T(8,128)S(1)} %copy.102), kind=kLoop, calls=%fused_computation.8 | loop fusion | flops 3014656 | bytes 2363392 | tf_op jit(solution)/shard_map/reduce_sum | solution.py:111
  (20 shorter events, 0.3 us)
Async XLA Ops:
  7.2 204.3 %copy-start = (bf16[2,768,4,128]{3,2,1,0:T(4,128)(2,1)S(1)}, bf16[2,768,4,128]{3,2,1,0:T(4,128)(2,1)}, u32[]{:S(2)}) copy-start(bf16[2,768,4,128]{3,2,1,0:T(4,128)(2,1)} %param.19) | copy-start | bytes 4718596
  7.2 21.6 %all-gather.2.cloned.1.call-start = ((), (), s32[]{:S(2)}) async-start(), calls=%async_computation.1 | async-start | bytes 1310720 | tf_op jit(solution)/shard_map/all_gather | solution.py:62
  7.9 160.1 %all-reduce.4.cloned.1.call-start = ((), (), s32[]{:S(2)}) async-start(), calls=%async_computation.2 | async-start | bytes 6291456 | tf_op jit(solution)/shard_map/psum | solution.py:97
  35.4 5.4 %copy-start.1 = (bf16[1024,1024]{1,0:T(8,128)(2,1)S(1)}, bf16[1024,1024]{1,0:T(8,128)(2,1)}, u32[]{:S(2)}) copy-start(bf16[1024,1024]{1,0:T(8,128)(2,1)} %gather_fusion) | copy-start | bytes 6291460
  190.0 5.8 %copy-start.2 = (s32[128,8]{0,1:T(8,128)S(1)}, s32[128,8]{0,1:T(8,128)}, u32[]{:S(2)}) copy-start(s32[128,8]{0,1:T(8,128)} %param.13) | copy-start | bytes 12292
  190.0 53.1 %all-to-all-start = ((bf16[4,4,128,1024]{3,2,1,0:T(8,128)(2,1)}), bf16[4,4,128,1024]{3,2,1,0:T(8,128)(2,1)}, u32[]{:S(2)}, u32[]{:S(2)}) async-start(bf16[4,4,128,1024]{3,2,1,0:T(8,128)(2,1)} %bitcast.47), calls=%async_computation | async-start | bytes 8388608 | tf_op jit(solution)/shard_map/all_to_all | solution.py:105
  204.0 7.3 %copy-start.4 = (bf16[128,8]{0,1:T(8,128)(2,1)S(1)}, bf16[128,8]{0,1:T(8,128)(2,1)}, u32[]{:S(2)}) copy-start(bf16[128,8]{0,1:T(8,128)(2,1)} %param.14) | copy-start | bytes 6148
  204.0 7.4 %copy-start.5 = (s32[2]{0:T(128)S(1)}, s32[2]{0:T(128)}, u32[]{:S(2)}) copy-start(s32[2]{0:T(128)} %param.21) | copy-start | bytes 28
  204.0 7.4 %copy-start.3 = (bf16[2,64,128]{2,1,0:T(8,128)(2,1)S(1)}, bf16[2,64,128]{2,1,0:T(8,128)(2,1)}, u32[]{:S(2)}) copy-start(bf16[2,64,128]{2,1,0:T(8,128)(2,1)} %param.18) | copy-start | bytes 98308
Sparse Core Ops, SparseCore 0:
  9.5 19.1 all-gather.1
  47.5 120.4 all-reduce.3
where the time goes:
time: 264 us; the launch traced here: 262 us
  waiting for transfers between devices  153 us (58%)
  local copies, waits for them, and re-layouts  54.7 us (21%)
  matrix products  17.1 us (6%)
  between operations  14.3 us (5%)
  other arithmetic  11.2 us (4%)
  blocking collectives  6.26 us (2%)
  starting transfers between devices  5.86 us (2%)
    psum x1, waiting for transfers between devices, body(): lax.psum(both_parts.astype(jnp.bfloat16), 'expert').astype(jnp.float32)  120 us
    all_to_all x1, waiting for transfers between devices, body(): lax.all_to_all(back_rows, 'attn', split_axis=0, concat_axis=0, tiled=True)  28.4 us
    gather x1, local copies, waits for them, and re-layouts, return_slots(): return pad_rows(results)[row_index]  12.9 us
    gather x1, local copies, waits for them, and re-layouts, body(): returned.reshape(experts * slot_count, feat_width)  8.78 us
    scatter x1, local copies, waits for them, and re-layouts, body(): pack_index = jnp.full((local_experts * capacity,), all_rows, jnp.int32).a...  8.04 us
    gather x5, local copies, waits for them, and re-layouts, body(): place_of = jnp.take_along_axis(position, expert_ids, axis=1)  7.39 us
    gather x3, local copies, waits for them, and re-layouts, body(): slot_of = jnp.take_along_axis(local_rank, expert_ids, axis=1)  7.2 us
    all_gather x1, blocking collectives, body(): lax.all_gather(expert_ids, 'attn', axis=0, tiled=True)  6.26 us
  transfers between devices with their start and end apart: 3, of which 3 were waited for; matrix products, arithmetic and copies ran while one was open for 11% of the time, Pallas kernels for 0%

commit v1 on v0

v1 whole, which is shorter than its diff:
```python
import functools

import jax
import jax.numpy as jnp
from jax import lax
from jax.experimental import pallas as pl
from jax.experimental.pallas import tpu as pltpu
from jax.sharding import PartitionSpec as P

F32 = jnp.float32
BF16 = jnp.bfloat16


def remote(src, dst, send_sem, recv_sem, axis, peer):
    return pltpu.make_async_remote_copy(
        src_ref=src,
        dst_ref=dst,
        send_sem=send_sem,
        recv_sem=recv_sem,
        device_id={axis: peer},
        device_id_type=pl.DeviceIdType.MESH,
    )


def moe_kernel(
    n_attn,
    n_exp,
    experts,
    tok_ref,
    meta_ref,
    wg_hbm,
    wu_hbm,
    wd_hbm,
    out_ref,
    wg,
    wu,
    wd,
    tok_all,
    meta_all,
    pos_col,
    pos_row,
    part,
    part_in,
    hid,
    acc,
    ret,
    ret_in,
    w_sem,
    tok_s,
    tok_r,
    meta_s,
    meta_r,
    part_s,
    part_r,
    hid_s,
    hid_r,
    ret_s,
    ret_r,
):
    me = lax.axis_index("attn")
    mine = lax.axis_index("expert")
    local = wg.shape[0]
    rows = tok_ref.shape[0]
    feat = tok_ref.shape[1]
    width = meta_ref.shape[1]
    ffn = wg.shape[2]
    slots = part.shape[2]
    capacity = n_exp * slots
    all_rows = n_attn * rows

    def weight_copy(i, j):
        src, dst = ((wg_hbm, wg), (wu_hbm, wu), (wd_hbm, wd))[i]
        return pltpu.make_async_copy(src.at[j], dst.at[j], w_sem.at[i, j])

    for j in range(local):
        weight_copy(0, j).start()
        weight_copy(1, j).start()
    for j in range(local):
        weight_copy(2, j).start()

    barrier = pltpu.get_barrier_semaphore()
    for d in range(1, n_attn):
        pl.semaphore_signal(
            barrier, inc=1, device_id={"attn": lax.rem(me + d, n_attn)},
            device_id_type=pl.DeviceIdType.MESH,
        )
    for d in range(1, n_exp):
        pl.semaphore_signal(
            barrier, inc=1, device_id={"expert": lax.rem(mine + d, n_exp)},
            device_id_type=pl.DeviceIdType.MESH,
        )
    pl.semaphore_wait(barrier, n_attn + n_exp - 2)

    def meta_copy(d, slot):
        return remote(meta_ref, meta_all.at[slot], meta_s.at[d - 1], meta_r.at[d - 1],
                      "attn", lax.rem(me + d, n_attn))

    def tok_copy(d, slot):
        return remote(tok_ref, tok_all.at[slot], tok_s.at[d - 1], tok_r.at[d - 1],
                      "attn", lax.rem(me + d, n_attn))

    for d in range(1, n_attn):
        meta_copy(d, me).start()
    for d in range(1, n_attn):
        tok_copy(d, me).start()
    tok_all[me] = tok_ref[...]
    meta_all[me] = meta_ref[...]
    for d in range(1, n_attn):
        meta_copy(d, lax.rem(me + n_attn - d, n_attn)).wait_recv()

    below = (
        lax.broadcasted_iota(jnp.int32, (rows, rows), 0)
        > lax.broadcasted_iota(jnp.int32, (rows, rows), 1)
    ).astype(F32).astype(BF16)
    offset = jnp.zeros((1, width), F32)
    for b in range(n_attn):
        block = meta_all[b]
        place = jnp.dot(below, block, preferred_element_type=F32) + offset
        wide = block.astype(F32)
        offset = offset + jnp.sum(wide, axis=0, keepdims=True)
        place = jnp.where(wide > 0.5, place, -1.0)
        pos_col[b] = place
        pos_row[:, b * rows:(b + 1) * rows] = place.T

    for d in range(1, n_attn):
        tok_copy(d, lax.rem(me + n_attn - d, n_attn)).wait_recv()

    def part_copy(j, d):
        peer = lax.rem(mine + d, n_exp)
        return remote(part.at[j, peer], part_in.at[j, d - 1], part_s.at[j, d - 1],
                      part_r.at[j, d - 1], "expert", peer)

    def hid_copy(j, d, slot):
        return remote(hid.at[j, mine], hid.at[j, slot], hid_s.at[j, d - 1],
                      hid_r.at[j, d - 1], "expert", lax.rem(mine + d, n_exp))

    def first(j, carry):
        place = pos_row[pl.ds(me * local + j, 1), :].astype(jnp.int32)
        chosen = lax.broadcasted_iota(jnp.int32, (capacity, all_rows), 0) == place
        packed = jnp.dot(
            chosen.astype(F32).astype(BF16),
            tok_all[...].reshape(all_rows, feat),
            preferred_element_type=F32,
        ).astype(BF16)
        weight_copy(0, j).wait()
        weight_copy(1, j).wait()
        gate = jnp.dot(packed, wg[j], preferred_element_type=F32).astype(BF16)
        part[j, :, :, :ffn] = gate.reshape(n_exp, slots, ffn)
        up = jnp.dot(packed, wu[j], preferred_element_type=F32).astype(BF16)
        part[j, :, :, ffn:] = up.reshape(n_exp, slots, ffn)
        for d in range(1, n_exp):
            part_copy(j, d).start()
        return carry

    lax.fori_loop(0, local, first, 0)

    def second(j, carry):
        for d in range(1, n_exp):
            part_copy(j, d).wait_recv()
        both = part[j, mine].astype(F32)
        for d in range(1, n_exp):
            both = both + part_in[j, d - 1].astype(F32)
        gate = both[:, :ffn]
        hid[j, mine] = (gate / (1.0 + jnp.exp(-gate)) * both[:, ffn:]).astype(BF16)
        for d in range(1, n_exp):
            hid_copy(j, d, mine).start()
        return carry

    lax.fori_loop(0, local, second, 0)

    acc[...] = jnp.zeros_like(acc)

    def third(j, carry):
        for d in range(1, n_exp):
            hid_copy(j, d, lax.rem(mine + n_exp - d, n_exp)).wait_recv()
        weight_copy(2, j).wait()
        result = jnp.dot(
            hid[j].reshape(capacity, ffn), wd[j], preferred_element_type=F32
        ).astype(BF16)
        column = me * local + j
        lanes = lax.broadcasted_iota(jnp.int32, (rows, width), 1)
        slot_ids = lax.broadcasted_iota(jnp.int32, (rows, capacity), 1)

        def combine(b, inner):
            place = jnp.sum(
                jnp.where(lanes == column, pos_col[b], 0.0), axis=1, keepdims=True
            ).astype(jnp.int32)
            factor = jnp.sum(
                jnp.where(lanes == column + experts, meta_all[b].astype(F32), 0.0),
                axis=1, keepdims=True,
            )
            spread = jnp.where(slot_ids == place, factor, 0.0).astype(BF16)
            acc[b] = acc[b] + jnp.dot(spread, result, preferred_element_type=F32)
            return inner

        for b in range(n_attn):
            combine(b, 0)
        return carry

    lax.fori_loop(0, local, third, 0)

    ret[...] = acc[...].astype(BF16)

    def ret_copy(d):
        peer = lax.rem(me + d, n_attn)
        return remote(ret.at[peer], ret_in.at[d - 1], ret_s.at[d - 1], ret_r.at[d - 1],
                      "attn", peer)

    for d in range(1, n_attn):
        ret_copy(d).start()
    total = acc[me]
    for d in range(1, n_attn):
        ret_copy(d).wait_recv()
        total = total + ret_in[d - 1].astype(F32)
    out_ref[...] = total.astype(BF16)

    for d in range(1, n_attn):
        meta_copy(d, me).wait_send()
        tok_copy(d, me).wait_send()
        ret_copy(d).wait_send()

    def drain(j, carry):
        for d in range(1, n_exp):
            part_copy(j, d).wait_send()
            hid_copy(j, d, mine).wait_send()
        return carry

    lax.fori_loop(0, local, drain, 0)


def routed(tokens, expert_ids, gate_weight, w_gate, w_up, w_down, n_attn, n_exp):
    rows, feat = tokens.shape
    local, _, ffn = w_gate.shape
    feat_out = w_down.shape[2]
    experts = local * n_attn
    capacity = rows * expert_ids.shape[1] // local
    slots = capacity // n_exp
    width = -(-2 * experts // 128) * 128
    wanted = jnp.arange(width, dtype=jnp.int32)[None, None, :]
    ids = expert_ids[:, :, None]
    gates = gate_weight.astype(F32)[:, :, None]
    meta = jnp.sum(
        jnp.where(ids == wanted, 1.0, jnp.where(ids + experts == wanted, gates, 0.0)),
        axis=1,
    ).astype(BF16)
    dma = pltpu.SemaphoreType.DMA
    vmem = pltpu.VMEM
    return pl.pallas_call(
        functools.partial(moe_kernel, n_attn, n_exp, experts),
        out_shape=jax.ShapeDtypeStruct((rows, feat_out), BF16),
        in_specs=[pl.BlockSpec(memory_space=pltpu.VMEM)] * 2
        + [pl.BlockSpec(memory_space=pl.ANY)] * 3,
        out_specs=pl.BlockSpec(memory_space=pltpu.VMEM),
        scratch_shapes=[
            vmem(w_gate.shape, BF16),
            vmem(w_up.shape, BF16),
            vmem(w_down.shape, BF16),
            vmem((n_attn, rows, feat), BF16),
            vmem((n_attn, rows, width), BF16),
            vmem((n_attn, rows, width), F32),
            vmem((width, n_attn * rows), F32),
            vmem((local, n_exp, slots, 2 * ffn), BF16),
            vmem((local, n_exp - 1, slots, 2 * ffn), BF16),
            vmem((local, n_exp, slots, ffn), BF16),
            vmem((n_attn, rows, feat_out), F32),
            vmem((n_attn, rows, feat_out), BF16),
            vmem((n_attn - 1, rows, feat_out), BF16),
            dma((3, local)),
            dma((n_attn - 1,)),
            dma((n_attn - 1,)),
            dma((n_attn - 1,)),
            dma((n_attn - 1,)),
            dma((local, n_exp - 1)),
            dma((local, n_exp - 1)),
            dma((local, n_exp - 1)),
            dma((local, n_exp - 1)),
            dma((n_attn - 1,)),
            dma((n_attn - 1,)),
        ],
        compiler_params=pltpu.CompilerParams(
            collective_id=0, has_side_effects=True, vmem_limit_bytes=52 * 1024 * 1024
        ),
    )(tokens, meta, w_gate, w_up, w_down)


def grouped_attention(query, cache_k, cache_v, lengths):
    seq_count, head_total, head_size = query.shape
    context = cache_k.shape[1]
    kv_count = cache_k.shape[2]
    grouped = query.reshape(seq_count, kv_count, head_total // kv_count, head_size)
    scores = jnp.einsum(
        "skgd,slkd->skgl", grouped, cache_k, preferred_element_type=jnp.float32
    ) * head_size ** (-0.5)
    live_mask = (
        lax.broadcasted_iota(jnp.int32, (seq_count, 1, 1, context), 3)
        < lengths[:, None, None, None]
    )
    masked = jnp.where(live_mask, scores, -jnp.inf)
    row_peak = jnp.max(masked, axis=3, keepdims=True)
    weighted = jnp.exp(masked - row_peak)
    denominator = jnp.sum(weighted, axis=3, keepdims=True)
    prob_bf = (weighted / denominator).astype(jnp.bfloat16)
    attended = jnp.einsum("skgl,slkd->skgd", prob_bf, cache_v, preferred_element_type=jnp.float32)
    return attended.reshape(seq_count, head_total * head_size).astype(jnp.bfloat16)


def body(tokens, expert_ids, gate_weight, w_gate, w_up, w_down, query, cache_k, cache_v, lengths):
    n_attn = lax.axis_size("attn")
    n_exp = lax.axis_size("expert")
    moe_out = routed(
        tokens, expert_ids, gate_weight, w_gate, w_up, w_down, n_attn, n_exp
    )
    attn_out = grouped_attention(query, cache_k, cache_v, lengths)
    return (moe_out, attn_out)


def solution(mesh):
    return jax.shard_map(
        body,
        mesh=mesh,
        in_specs=(
            P(("groups", "attn"), "expert"),
            P(("groups", "attn"), None),
            P(("groups", "attn"), None),
            P("attn", "expert", None),
            P("attn", "expert", None),
            P("attn", None, "expert"),
            P(("groups", "attn", "expert"), None, None),
            P(("groups", "attn", "expert"), None, None, None),
            P(("groups", "attn", "expert"), None, None, None),
            P(("groups", "attn", "expert")),
        ),
        out_specs=(P(("groups", "attn"), "expert"), P(("groups", "attn", "expert"), None)),
        check_vma=False,
    )
```

time: 264 us -> 140 us (0.53)
  waiting for transfers between devices: 153 us -> 0 us
  Pallas kernels: 0 us -> 131 us
  local copies, waits for them, and re-layouts: 54.7 us -> 2.27 us
  matrix products: 17.1 us -> 3.15 us
  between operations: 14.3 us -> 0.7 us
  other arithmetic: 11.2 us -> 1.85 us
  blocking collectives: 6.26 us -> 0 us
  starting transfers between devices: 5.86 us -> 0 us
    pallas_call x0 -> x1, Pallas kernels: none -> 131 us  [routed(): pl.pallas_call(functools.partial(moe_kernel, n_attn, n_exp, experts), out...]
    psum x1 -> x0, waiting for transfers between devices: 120 us -> none  [body(): lax.psum(both_parts.astype(jnp.bfloat16), 'expert').astype(jnp.float32)]
    gather x11 -> x0, local copies, waits for them, and re-layouts: 41.6 us -> none  [the longest x1 12.9 us: return_slots(): return pad_rows(results)[row_index]]
    all_to_all x1 -> x0, waiting for transfers between devices: 28.4 us -> none  [body(): lax.all_to_all(back_rows, 'attn', split_axis=0, concat_axis=0, tiled=True)]
    dot_general x3 -> x0, matrix products: 14.8 us -> none  [the longest x1 5.35 us: body(): jnp.einsum('jrd,jdf->jrf', packed, w_up, preferred_element_type=jnp.float32)]
    scatter x1 -> x0, local copies, waits for them, and re-layouts: 8.04 us -> none  [body(): pack_index = jnp.full((local_experts * capacity,), all_rows, jnp.int32).a...]
    all_gather x1 -> x0, blocking collectives: 6.26 us -> none  [body(): lax.all_gather(expert_ids, 'attn', axis=0, tiled=True)]
    all_to_all x1 -> x0, starting transfers between devices: 5.78 us -> none  [body(): lax.all_to_all(back_rows, 'attn', split_axis=0, concat_axis=0, tiled=True)]
  transfers between devices with their start and end apart: 3 -> 0, of which waited for: 3 -> 0; matrix products, arithmetic and copies ran while one was open for 11% -> 0% of each run, Pallas kernels for 0% -> 0%
where the time goes in v1:
time: 140 us; the launch traced here: 139 us
  Pallas kernels  131 us (94%)
  matrix products  3.15 us (2%)
  local copies, waits for them, and re-layouts  2.27 us (2%)
  other arithmetic  1.85 us (1%)
    pallas_call x1, Pallas kernels, routed(): pl.pallas_call(functools.partial(moe_kernel, n_attn, n_exp, experts), out...  131 us

profile of v1, /device:TPU:1, one launch (start us, length us, event | category | flops | bytes accessed | tf_op | source)
XLA Modules:
  0.0 139.4 jit_solution(10228234220454686078)
XLA Ops:
  0.6 0.0 copy-start
  0.6 0.8 iota_compare_fusion.2
  1.5 0.6 copy-done
  2.1 1.3 fusion.10
  3.3 0.2 fusion.18
  3.6 0.0 copy-start.2
  3.6 0.0 copy-start.3
  3.6 0.0 copy-start.1
  3.6 1.9 %fusion.13 = bf16[2,4,16,128]{3,2,1,0:T(8,128)(2,1)S(1)} fusion(bf16[2,768,4,128]{3,2,1,0:T(4,128)(2,1)} %param.18, f32[2,4,16]{2,1,0:T(4,128)S(1)} %fusion.18, f32[2,4,16,768]{3,2,1,0:T(8,128)S(1)} %fusion.10), kind=kOutput, calls=%fused_computation.9 | convolution fusion | flops 25478016 | bytes 1999360 | tf_op jit(solution)/shard_map/skgl,slkd->skgd/dot_general | solution.py:303
  5.5 0.7 copy.34
  6.2 0.0 copy-done.2
  6.2 0.1 copy.18
  6.3 0.1 copy.17
  6.4 0.0 copy-done.3
  6.4 0.1 copy.19
  6.5 0.8 select_reduce_fusion.meta_ref
  7.2 0.0 copy-done.1
  7.3 131.5 %shard_map.113 = bf16[128,1024]{1,0:T(8,128)(2,1)S(1)} custom-call(bf16[128,1024]{1,0:T(8,128)(2,1)S(1)} %copy-done.1, bf16[128,128]{1,0:T(8,128)(2,1)S(1)} %select_reduce_fusion.meta_ref, bf16[4,1024,768]{2,1,0:T(8,128)(2,1)} %wg_hbm.1, bf16[4,1024,768]{2,1,0:T(8,128)(2,1)} %wu_hbm.1, bf16[4,768,1024]{2,1,0:T(8,128)(2,1)} %wd_hbm.1), custom_call_target="tpu_custom_call" | custom-call | tf_op jit(solution)/shard_map/pallas_call | solution.py:248
  138.7 0.7 copy.36
  (1 shorter events, 0.0 us)
Async XLA Ops:
  0.6 1.4 %copy-start = (bf16[2,768,4,128]{3,2,1,0:T(4,128)(2,1)S(1)}, bf16[2,768,4,128]{3,2,1,0:T(4,128)(2,1)}, u32[]{:S(2)}) copy-start(bf16[2,768,4,128]{3,2,1,0:T(4,128)(2,1)} %param.17) | copy-start | bytes 4718596
  3.6 2.6 %copy-start.2 = (s32[128,8]{0,1:T(8,128)S(1)}, s32[128,8]{0,1:T(8,128)}, u32[]{:S(2)}) copy-start(s32[128,8]{0,1:T(8,128)} %param.11) | copy-start | bytes 12292
  3.6 2.8 %copy-start.3 = (bf16[128,8]{0,1:T(8,128)(2,1)S(1)}, bf16[128,8]{0,1:T(8,128)(2,1)}, u32[]{:S(2)}) copy-start(bf16[128,8]{0,1:T(8,128)(2,1)} %param.12) | copy-start | bytes 6148
  3.6 3.6 %copy-start.1 = (bf16[128,1024]{1,0:T(8,128)(2,1)S(1)}, bf16[128,1024]{1,0:T(8,128)(2,1)}, u32[]{:S(2)}) copy-start(bf16[128,1024]{1,0:T(8,128)(2,1)} %tok_ref.1) | copy-start | bytes 786436

commit v2 on v1

--- a/solution.py
+++ b/solution.py
@@ -22,38 +22,71 @@
     )
 
 
+def attend(length_ref, query_ref, ck_ref, cv_ref, att_ref, kv_count):
+    seqs, heads, size = query_ref.shape
+    span = ck_ref.shape[1]
+    column = lax.broadcasted_iota(jnp.int32, (heads, span), 1)
+    row = lax.broadcasted_iota(jnp.int32, (heads, span), 0)
+    own = lax.rem(column, kv_count) == row // (heads // kv_count)
+    for s in range(seqs):
+        scores = lax.dot_general(
+            query_ref[s], ck_ref[s], (((1,), (1,)), ((), ())),
+            preferred_element_type=F32,
+        ) * size ** (-0.5)
+        live = own & (column < length_ref[s] * kv_count)
+        masked = jnp.where(live, scores, -jnp.inf)
+        peak = jnp.max(masked, axis=1, keepdims=True)
+        weighted = jnp.exp(masked - peak)
+        prob = (weighted / jnp.sum(weighted, axis=1, keepdims=True)).astype(BF16)
+        att_ref[s] = jnp.dot(prob, cv_ref[s], preferred_element_type=F32).astype(BF16)
+
+
 def moe_kernel(
     n_attn,
     n_exp,
     experts,
+    kv_count,
     tok_ref,
     meta_ref,
     wg_hbm,
     wu_hbm,
     wd_hbm,
+    length_ref,
+    query_ref,
+    ck_hbm,
+    cv_hbm,
     out_ref,
+    att_ref,
     wg,
     wu,
     wd,
+    ck,
+    cv,
     tok_all,
     meta_all,
     pos_col,
     pos_row,
     part,
+    pair_in,
     part_in,
     hid,
     acc,
     ret,
     ret_in,
     w_sem,
+    c_sem,
     tok_s,
     tok_r,
     meta_s,
     meta_r,
+    pair_s,
+    pair_r,
     part_s,
     part_r,
     hid_s,
     hid_r,
+    back_s,
+    back_r,
     ret_s,
     ret_r,
 ):
@@ -64,7 +97,9 @@
     feat = tok_ref.shape[1]
     width = meta_ref.shape[1]
     ffn = wg.shape[2]
-    slots = part.shape[2]
+    pairs, half, slots = part.shape[1:4]
+    side = lax.rem(mine, pairs)
+    place_in_half = mine // pairs
     capacity = n_exp * slots
     all_rows = n_attn * rows
 
@@ -77,6 +112,11 @@
         weight_copy(1, j).start()
     for j in range(local):
         weight_copy(2, j).start()
+
+    ck_copy = pltpu.make_async_copy(ck_hbm, ck, c_sem.at[0])
+    cv_copy = pltpu.make_async_copy(cv_hbm, cv, c_sem.at[1])
+    ck_copy.start()
+    cv_copy.start()
 
     barrier = pltpu.get_barrier_semaphore()
     for d in range(1, n_attn):
@@ -125,16 +165,30 @@
     for d in range(1, n_attn):
         tok_copy(d, lax.rem(me + n_attn - d, n_attn)).wait_recv()
 
+    def pair_copy(j):
+        return remote(part.at[j, 1 - side], pair_in.at[j], pair_s.at[j], pair_r.at[j],
+                      "expert", mine + 1 - 2 * side)
+
     def part_copy(j, d):
-        peer = lax.rem(mine + d, n_exp)
-        return remote(part.at[j, peer], part_in.at[j, d - 1], part_s.at[j, d - 1],
-                      part_r.at[j, d - 1], "expert", peer)
+        other = lax.rem(place_in_half + d, half)
+        return remote(part.at[j, side, other], part_in.at[j, d - 1], part_s.at[j, d - 1],
+                      part_r.at[j, d - 1], "expert", other * pairs + side)
 
     def hid_copy(j, d, slot):
-        return remote(hid.at[j, mine], hid.at[j, slot], hid_s.at[j, d - 1],
-                      hid_r.at[j, d - 1], "expert", lax.rem(mine + d, n_exp))
-
-    def first(j, carry):
+        other = lax.rem(place_in_half + d, half)
+        return remote(hid.at[j, side, place_in_half], hid.at[j, side, slot],
+                      hid_s.at[j, d - 1], hid_r.at[j, d - 1], "expert",
+                      other * pairs + side)
+
+    def hid_arrive(j):
+        for d in range(1, half):
+            hid_copy(j, d, lax.rem(place_in_half + half - d, half)).wait_recv()
+
+    def back_copy(j, which):
+        return remote(hid.at[j, side], hid.at[j, which], back_s.at[j], back_r.at[j],
+                      "expert", mine + 1 - 2 * side)
+
+    def first(j):
         place = pos_row[pl.ds(me * local + j, 1), :].astype(jnp.int32)
         chosen = lax.broadcasted_iota(jnp.int32, (capacity, all_rows), 0) == place
         packed = jnp.dot(
@@ -145,34 +199,42 @@
         weight_copy(0, j).wait()
         weight_copy(1, j).wait()
         gate = jnp.dot(packed, wg[j], preferred_element_type=F32).astype(BF16)
-        part[j, :, :, :ffn] = gate.reshape(n_exp, slots, ffn)
+        part[j, :, :, :, :ffn] = gate.reshape(pairs, half, slots, ffn)
         up = jnp.dot(packed, wu[j], preferred_element_type=F32).astype(BF16)
-        part[j, :, :, ffn:] = up.reshape(n_exp, slots, ffn)
-        for d in range(1, n_exp):
+        part[j, :, :, :, ffn:] = up.reshape(pairs, half, slots, ffn)
+        if pairs > 1:
+            pair_copy(j).start()
+
+    def reduce_pair(j):
+        if pairs > 1:
+            pair_copy(j).wait_recv()
+            part[j, side] = (part[j, side].astype(F32) + pair_in[j].astype(F32)).astype(BF16)
+        for d in range(1, half):
             part_copy(j, d).start()
-        return carry
-
-    lax.fori_loop(0, local, first, 0)
-
-    def second(j, carry):
-        for d in range(1, n_exp):
+
+    def second(j):
+        for d in range(1, half):
             part_copy(j, d).wait_recv()
-        both = part[j, mine].astype(F32)
-        for d in range(1, n_exp):
+        both = part[j, side, place_in_half].astype(F32)
+        for d in range(1, half):
             both = both + part_in[j, d - 1].astype(F32)
         gate = both[:, :ffn]
-        hid[j, mine] = (gate / (1.0 + jnp.exp(-gate)) * both[:, ffn:]).astype(BF16)
-        for d in range(1, n_exp):
-            hid_copy(j, d, mine).start()
-        return carry
-
-    lax.fori_loop(0, local, second, 0)
+        hid[j, side, place_in_half] = (
+            gate / (1.0 + jnp.exp(-gate)) * both[:, ffn:]
+        ).astype(BF16)
+        for d in range(1, half):
+            hid_copy(j, d, place_in_half).start()
+
+    def pass_on(j):
+        hid_arrive(j)
+        if pairs > 1:
+            back_copy(j, side).start()
 
     acc[...] = jnp.zeros_like(acc)
 
-    def third(j, carry):
-        for d in range(1, n_exp):
-            hid_copy(j, d, lax.rem(mine + n_exp - d, n_exp)).wait_recv()
+    def third(j):
+        if pairs > 1:
+            back_copy(j, 1 - side).wait_recv()
         weight_copy(2, j).wait()
         result = jnp.dot(
             hid[j].reshape(capacity, ffn), wd[j], preferred_element_type=F32
@@ -195,9 +257,22 @@
 
         for b in range(n_attn):
             combine(b, 0)
+
+    def step(s, carry):
+        for lag, stage in enumerate((first, reduce_pair, second, pass_on, third)):
+            if lag == 2:
+                @pl.when(s == 1)
+                def _():
+                    attend(length_ref, query_ref, ck, cv, att_ref, kv_count)
+
+            @pl.when((s >= lag) & (s < local + lag))
+            def _():
+                stage(s - lag)
         return carry
 
-    lax.fori_loop(0, local, third, 0)
+    ck_copy.wait()
+    cv_copy.wait()
+    lax.fori_loop(0, local + 4, step, 0)
 
     ret[...] = acc[...].astype(BF16)
 
@@ -220,21 +295,26 @@
         ret_copy(d).wait_send()
 
     def drain(j, carry):
-        for d in range(1, n_exp):
+        if pairs > 1:
+            pair_copy(j).wait_send()
+            back_copy(j, side).wait_send()
+        for d in range(1, half):
             part_copy(j, d).wait_send()
-            hid_copy(j, d, mine).wait_send()
+            hid_copy(j, d, place_in_half).wait_send()
         return carry
 
     lax.fori_loop(0, local, drain, 0)
 
 
-def routed(tokens, expert_ids, gate_weight, w_gate, w_up, w_down, n_attn, n_exp):
+def routed(tokens, expert_ids, gate_weight, w_gate, w_up, w_down, query, cache_k, cache_v, lengths, n_attn, n_exp):
     rows, feat = tokens.shape
     local, _, ffn = w_gate.shape
     feat_out = w_down.shape[2]
     experts = local * n_attn
     capacity = rows * expert_ids.shape[1] // local
     slots = capacity // n_exp
+    pairs = 2 if n_exp > 2 and n_exp % 2 == 0 else 1
+    half = n_exp // pairs
     width = -(-2 * experts // 128) * 128
     wanted = jnp.arange(width, dtype=jnp.int32)[None, None, :]
     ids = expert_ids[:, :, None]
@@ -243,74 +323,74 @@
         jnp.where(ids == wanted, 1.0, jnp.where(ids + experts == wanted, gates, 0.0)),
         axis=1,
     ).astype(BF16)
+    seqs, heads, size = query.shape
+    context, kv_count = cache_k.shape[1:3]
+    flat = (seqs, context * kv_count, size)
     dma = pltpu.SemaphoreType.DMA
     vmem = pltpu.VMEM
     return pl.pallas_call(
-        functools.partial(moe_kernel, n_attn, n_exp, experts),
-        out_shape=jax.ShapeDtypeStruct((rows, feat_out), BF16),
+        functools.partial(moe_kernel, n_attn, n_exp, experts, kv_count),
+        out_shape=(
+            jax.ShapeDtypeStruct((rows, feat_out), BF16),
+            jax.ShapeDtypeStruct(query.shape, BF16),
+        ),
         in_specs=[pl.BlockSpec(memory_space=pltpu.VMEM)] * 2
-        + [pl.BlockSpec(memory_space=pl.ANY)] * 3,
-        out_specs=pl.BlockSpec(memory_space=pltpu.VMEM),
+        + [pl.BlockSpec(memory_space=pl.ANY)] * 3
+        + [pl.BlockSpec(memory_space=pltpu.SMEM)]
+        + [pl.BlockSpec(memory_space=pltpu.VMEM)]
+        + [pl.BlockSpec(memory_space=pl.ANY)] * 2,
+        out_specs=[pl.BlockSpec(memory_space=pltpu.VMEM)] * 2,
         scratch_shapes=[
             vmem(w_gate.shape, BF16),
             vmem(w_up.shape, BF16),
             vmem(w_down.shape, BF16),
+            vmem(flat, BF16),
+            vmem(flat, BF16),
             vmem((n_attn, rows, feat), BF16),
             vmem((n_attn, rows, width), BF16),
             vmem((n_attn, rows, width), F32),
             vmem((width, n_attn * rows), F32),
-            vmem((local, n_exp, slots, 2 * ffn), BF16),
-            vmem((local, n_exp - 1, slots, 2 * ffn), BF16),
-            vmem((local, n_exp, slots, ffn), BF16),
+            vmem((local, pairs, half, slots, 2 * ffn), BF16),
+            vmem((local, half, slots, 2 * ffn), BF16),
+            vmem((local, half - 1, slots, 2 * ffn), BF16),
+            vmem((local, pairs, half, slots, ffn), BF16),
             vmem((n_attn, rows, feat_out), F32),
             vmem((n_attn, rows, feat_out), BF16),
             vmem((n_attn - 1, rows, feat_out), BF16),
             dma((3, local)),
-            dma((n_attn - 1,)),
-            dma((n_attn - 1,)),
-            dma((n_attn - 1,)),
-            dma((n_attn - 1,)),
-            dma((local, n_exp - 1)),
-            dma((local, n_exp - 1)),
-            dma((local, n_exp - 1)),
-            dma((local, n_exp - 1)),
+            dma((2,)),
+            dma((n_attn - 1,)),
+            dma((n_attn - 1,)),
+            dma((n_attn - 1,)),
+            dma((n_attn - 1,)),
+            dma((local,)),
+            dma((local,)),
+            dma((local, half - 1)),
+            dma((local, half - 1)),
+            dma((local, half - 1)),
+            dma((local, half - 1)),
+            dma((local,)),
+            dma((local,)),
             dma((n_attn - 1,)),
             dma((n_attn - 1,)),
         ],
         compiler_params=pltpu.CompilerParams(
             collective_id=0, has_side_effects=True, vmem_limit_bytes=52 * 1024 * 1024
         ),
-    )(tokens, meta, w_gate, w_up, w_down)
-
-
-def grouped_attention(query, cache_k, cache_v, lengths):
-    seq_count, head_total, head_size = query.shape
-    context = cache_k.shape[1]
-    kv_count = cache_k.shape[2]
-    grouped = query.reshape(seq_count, kv_count, head_total // kv_count, head_size)
-    scores = jnp.einsum(
-        "skgd,slkd->skgl", grouped, cache_k, preferred_element_type=jnp.float32
-    ) * head_size ** (-0.5)
-    live_mask = (
-        lax.broadcasted_iota(jnp.int32, (seq_count, 1, 1, context), 3)
-        < lengths[:, None, None, None]
+    )(
+        tokens, meta, w_gate, w_up, w_down, lengths, query,
+        cache_k.reshape(flat), cache_v.reshape(flat),
     )
-    masked = jnp.where(live_mask, scores, -jnp.inf)
-    row_peak = jnp.max(masked, axis=3, keepdims=True)
-    weighted = jnp.exp(masked - row_peak)
-    denominator = jnp.sum(weighted, axis=3, keepdims=True)
-    prob_bf = (weighted / denominator).astype(jnp.bfloat16)
-    attended = jnp.einsum("skgl,slkd->skgd", prob_bf, cache_v, preferred_element_type=jnp.float32)
-    return attended.reshape(seq_count, head_total * head_size).astype(jnp.bfloat16)
 
 
 def body(tokens, expert_ids, gate_weight, w_gate, w_up, w_down, query, cache_k, cache_v, lengths):
     n_attn = lax.axis_size("attn")
     n_exp = lax.axis_size("expert")
-    moe_out = routed(
-        tokens, expert_ids, gate_weight, w_gate, w_up, w_down, n_attn, n_exp
+    moe_out, attended = routed(
+        tokens, expert_ids, gate_weight, w_gate, w_up, w_down,
+        query, cache_k, cache_v, lengths, n_attn, n_exp,
     )
-    attn_out = grouped_attention(query, cache_k, cache_v, lengths)
+    attn_out = attended.reshape(query.shape[0], -1)
     return (moe_out, attn_out)
 
 

time: 140 us -> 114 us (0.81)
  Pallas kernels: 131 us -> 106 us
  matrix products: 3.15 us -> 0 us
  local copies, waits for them, and re-layouts: 2.27 us -> 5.38 us
    pallas_call x1, Pallas kernels: 131 us -> 106 us  [routed(): pl.pallas_call(functools.partial(moe_kernel, n_attn, n_exp, experts, kv_c...]
    dot_general x2 -> x0, matrix products: 3.15 us -> none  [the longest x1 1.88 us: grouped_attention(): jnp.einsum('skgl,slkd->skgd', prob_bf, cache_v, preferred_element_type=jn...]
    unnamed x11 -> x9, local copies, waits for them, and re-layouts: 2.06 us -> 4.5 us
where the time goes in v2:
time: 114 us; the launch traced here: 113 us
  Pallas kernels  106 us (93%)
  local copies, waits for them, and re-layouts  5.38 us (5%)
  other arithmetic  1.45 us (1%)
    pallas_call x1, Pallas kernels, routed(): pl.pallas_call(functools.partial(moe_kernel, n_attn, n_exp, experts, kv_c...  106 us
    unnamed x9, local copies, waits for them, and re-layouts  4.5 us

profile of v2, /device:TPU:1, one launch (start us, length us, event | category | flops | bytes accessed | tf_op | source)
XLA Modules:
  0.0 113.2 jit_solution(14589166979852905383)
XLA Ops:
  0.6 0.7 broadcast_add_fusion
  1.3 0.1 copy.16
  1.4 0.8 copy.17
  2.2 0.8 copy.15
  3.0 0.8 select_reduce_fusion.meta_ref
  3.8 0.0 copy-start
  3.8 0.9 copy-done
  4.7 0.0 copy-start.1
  4.7 0.8 copy-done.1
  5.5 0.0 copy-start.2
  5.5 0.7 copy-done.2
  6.1 105.7 %shard_map.113 = (bf16[128,1024]{1,0:T(8,128)(2,1)S(1)}, bf16[2,64,128]{2,1,0:T(8,128)(2,1)S(1)}) custom-call(bf16[128,1024]{1,0:T(8,128)(2,1)S(1)} %copy-done, bf16[128,128]{1,0:T(8,128)(2,1)S(1)} %select_reduce_fusion.meta_ref, bf16[4,1024,768]{2,1,0:T(8,128)(2,1)} %wg_hbm.1, bf16[4,1024,768]{2,1,0:T(8,128)(2,1)} %wu_hbm.1, bf16[4,768,1024]{2,1,0:T(8,128)(2,1)} %wd_hbm.1, ...), custom_call_target="tpu_custom_call" | custom-call | tf_op jit(solution)/shard_map/pallas_call | solution.py:331
  111.8 0.6 copy.20
  112.5 0.7 copy.22
Async XLA Ops:
  3.8 1.0 copy-start
  4.7 0.8 copy-start.1
  5.5 0.7 copy-start.2

commit v3 on v2

--- a/solution.py
+++ b/solution.py
@@ -135,14 +135,24 @@
         return remote(meta_ref, meta_all.at[slot], meta_s.at[d - 1], meta_r.at[d - 1],
                       "attn", lax.rem(me + d, n_attn))
 
+    chips = n_attn // 2
+    twin = me + 1 - 2 * lax.rem(me, 2)
+
     def tok_copy(d, slot):
         return remote(tok_ref, tok_all.at[slot], tok_s.at[d - 1], tok_r.at[d - 1],
-                      "attn", lax.rem(me + d, n_attn))
+                      "attn", lax.rem(me + 2 * d, n_attn))
+
+    def tok_twin(d, owner):
+        slot = lax.rem(owner + n_attn - 2 * d, n_attn)
+        src = tok_all.at[slot] if d else tok_ref
+        return remote(src, tok_all.at[slot], tok_s.at[chips - 1 + d],
+                      tok_r.at[chips - 1 + d], "attn", twin)
 
     for d in range(1, n_attn):
         meta_copy(d, me).start()
-    for d in range(1, n_attn):
+    for d in range(1, chips):
         tok_copy(d, me).start()
+    tok_twin(0, me).start()
     tok_all[me] = tok_ref[...]
     meta_all[me] = meta_ref[...]
     for d in range(1, n_attn):
@@ -162,8 +172,11 @@
         pos_col[b] = place
         pos_row[:, b * rows:(b + 1) * rows] = place.T
 
-    for d in range(1, n_attn):
-        tok_copy(d, lax.rem(me + n_attn - d, n_attn)).wait_recv()
+    for d in range(1, chips):
+        tok_copy(d, lax.rem(me + n_attn - 2 * d, n_attn)).wait_recv()
+        tok_twin(d, me).start()
+    for d in range(chips):
+        tok_twin(d, twin).wait_recv()
 
     def pair_copy(j):
         return remote(part.at[j, 1 - side], pair_in.at[j], pair_s.at[j], pair_r.at[j],
@@ -291,8 +304,12 @@
 
     for d in range(1, n_attn):
         meta_copy(d, me).wait_send()
+        ret_copy(d).wait_send()
+
+    for d in range(1, chips):
         tok_copy(d, me).wait_send()
-        ret_copy(d).wait_send()
+    for d in range(chips):
+        tok_twin(d, me).wait_send()
 
     def drain(j, carry):
         if pairs > 1:

time: 114 us -> 116 us (1.018)
  Pallas kernels: 106 us -> 108 us
    pallas_call x1, Pallas kernels: 106 us -> 108 us  [routed(): pl.pallas_call(functools.partial(moe_kernel, n_attn, n_exp, experts, kv_c...]
where the time goes in v3:
time: 116 us; the launch traced here: 115 us
  Pallas kernels  108 us (93%)
  local copies, waits for them, and re-layouts  5.38 us (5%)
  other arithmetic  1.45 us (1%)
    pallas_call x1, Pallas kernels, routed(): pl.pallas_call(functools.partial(moe_kernel, n_attn, n_exp, experts, kv_c...  108 us
    unnamed x9, local copies, waits for them, and re-layouts  4.5 us

profile of v3, /device:TPU:1, one launch (start us, length us, event | category | flops | bytes accessed | tf_op | source)
XLA Modules:
  0.0 115.4 jit_solution(17417479721497478818)
XLA Ops:
  0.6 0.7 broadcast_add_fusion
  1.3 0.1 copy.16
  1.4 0.8 copy.17
  2.2 0.8 copy.15
  3.0 0.8 select_reduce_fusion.meta_ref
  3.8 0.0 copy-start
  3.8 0.9 copy-done
  4.7 0.0 copy-start.1
  4.7 0.8 copy-done.1
  5.5 0.0 copy-start.2
  5.5 0.7 copy-done.2
  6.1 108.0 %shard_map.113 = (bf16[128,1024]{1,0:T(8,128)(2,1)S(1)}, bf16[2,64,128]{2,1,0:T(8,128)(2,1)S(1)}) custom-call(bf16[128,1024]{1,0:T(8,128)(2,1)S(1)} %copy-done, bf16[128,128]{1,0:T(8,128)(2,1)S(1)} %select_reduce_fusion.meta_ref, bf16[4,1024,768]{2,1,0:T(8,128)(2,1)} %wg_hbm.1, bf16[4,1024,768]{2,1,0:T(8,128)(2,1)} %wu_hbm.1, bf16[4,768,1024]{2,1,0:T(8,128)(2,1)} %wd_hbm.1, ...), custom_call_target="tpu_custom_call" | custom-call | tf_op jit(solution)/shard_map/pallas_call | solution.py:348
  114.1 0.6 copy.20
  114.7 0.7 copy.22
Async XLA Ops:
  3.8 1.0 copy-start
  4.7 0.8 copy-start.1
  5.5 0.7 copy-start.2
